TPU v7x, 8 devices: a whole 2x2x1 slice. The times are simulated.
8 devices in a mesh: data: 1 (over z), model: 8 (over y, x, core).
Axes of the slice: x: 2, y: 2, z: 1, core: 2. Of those that a mesh axis runs over, the one named last changes fastest.
Arguments:
- act_x: bfloat16 [1536, 5120], P('data')
- seg_ids: int32 [1536], P('data')
- gain_one: bfloat16 [5120], replicated
- gain_two: bfloat16 [5120], replicated
- w_qkv: bfloat16 [5120, 15360], P(None, 'model')
- w_out: bfloat16 [40, 128, 5120], P('model')
- w_up: bfloat16 [5120, 20480], P(None, 'model')
- w_down: bfloat16 [20480, 5120], P('model')
- grad_y: bfloat16 [1536, 5120], P('data')
Outputs:
- output 1: bfloat16 [1536, 5120], P('data')
- output 2: bfloat16 [1536, 5120], P('data')
- output 3: bfloat16 [5120, 15360], P('data', 'model')
- output 4: bfloat16 [40, 128, 5120], P(('data', 'model'))
- output 5: bfloat16 [5120, 20480], P('data', 'model')
- output 6: bfloat16 [20480, 5120], P(('data', 'model'))
- output 7: bfloat16 [5120], P('data')
- output 8: bfloat16 [5120], P('data')
All inputs are finite; a program needn't handle non-finite values.
Results may differ from a plain program's by a relative error of at most 0.02.
Values are sent between devices in bfloat16 or wider.
A program may use at most 1 GiB of HBM per device.

v0:
```python
import functools
import jax
import jax.numpy as jnp
from jax import lax
from jax.sharding import PartitionSpec as P

LN_EPS = 1e-5
gelu_tanh = functools.partial(jax.nn.gelu, approximate=True)


def normalize(values):
    values_f32 = values.astype(jnp.float32)
    centered = values_f32 - jnp.mean(values_f32, axis=-1, keepdims=True)
    inv_std = lax.rsqrt(jnp.mean(centered * centered, axis=-1, keepdims=True) + LN_EPS)
    return centered * inv_std, inv_std


def norm_backward(grad_out, x_hat, inv_std, gain_vec):
    d_gain = jnp.sum(grad_out * x_hat, axis=0)
    d_hat = grad_out * gain_vec.astype(jnp.float32)
    d_in = inv_std * (d_hat - jnp.mean(d_hat, axis=-1, keepdims=True)
                      - x_hat * jnp.mean(d_hat * x_hat, axis=-1, keepdims=True))
    return d_in, d_gain


def visible_keys(q_pos, k_pos, q_seg, k_seg):
    return (q_pos[:, None] >= k_pos[None, :]) & (q_seg[:, None] == k_seg[None, :])


def attention_fwd(q_rows, k_rows, v_rows, key_mask):
    q_scale = q_rows.shape[-1] ** -0.5
    scores = jnp.einsum("shd,thd->hst", q_rows, k_rows, preferred_element_type=jnp.float32) * q_scale
    scores = jnp.where(key_mask[None], scores, -1e30)
    prob_f32 = jax.nn.softmax(scores, axis=-1)
    prob_bf = prob_f32.astype(jnp.bfloat16)
    attn_rows = jnp.einsum("hst,thd->shd", prob_bf, v_rows, preferred_element_type=jnp.float32).astype(jnp.bfloat16)
    return attn_rows, prob_f32, prob_bf


def attention_bwd(d_rows, q_rows, k_rows, v_rows, prob_f32, prob_bf):
    q_scale = q_rows.shape[-1] ** -0.5
    d_prob = jnp.einsum("shd,thd->hst", d_rows, v_rows, preferred_element_type=jnp.float32)
    d_prob = d_prob.astype(jnp.bfloat16).astype(jnp.float32)
    d_scores = prob_f32 * (d_prob - jnp.sum(prob_f32 * d_prob, axis=-1, keepdims=True))
    d_scores = (d_scores * q_scale).astype(jnp.bfloat16)
    d_query = jnp.einsum("hst,thd->shd", d_scores, k_rows, preferred_element_type=jnp.float32).astype(jnp.bfloat16)
    d_key = jnp.einsum("hst,shd->thd", d_scores, q_rows, preferred_element_type=jnp.float32).astype(jnp.bfloat16)
    d_value = jnp.einsum("hst,shd->thd", prob_bf, d_rows, preferred_element_type=jnp.float32).astype(jnp.bfloat16)
    return d_query, d_key, d_value


def solution(mesh):
    def local_layer(act_x, seg_ids, gain_one, gain_two, w_qkv, w_out, w_up, w_down, grad_y):
        tokens = act_x.shape[0]
        local_heads, head_dim = w_out.shape[0], w_out.shape[1]
        positions = lax.iota(jnp.int32, tokens)
        key_mask = visible_keys(positions, positions, seg_ids, seg_ids)

        hat_one, inv_one = normalize(act_x)
        normed_one = (hat_one * gain_one.astype(jnp.float32)).astype(jnp.bfloat16)
        qkv_rows = jnp.dot(normed_one, w_qkv, preferred_element_type=jnp.float32).astype(jnp.bfloat16)
        qkv_rows = qkv_rows.reshape(tokens, local_heads, 3, head_dim)
        q_rows = qkv_rows[:, :, 0]
        k_rows = qkv_rows[:, :, 1]
        v_rows = qkv_rows[:, :, 2]
        attn_rows, prob_f32, prob_bf = attention_fwd(q_rows, k_rows, v_rows, key_mask)
        part_one = jnp.einsum("shd,hde->se", attn_rows, w_out, preferred_element_type=jnp.float32).astype(jnp.bfloat16)
        sum_one = lax.psum(part_one, "model")
        resid_rows = (act_x.astype(jnp.float32) + sum_one.astype(jnp.float32)).astype(jnp.bfloat16)
        hat_two, inv_two = normalize(resid_rows)
        normed_two = (hat_two * gain_two.astype(jnp.float32)).astype(jnp.bfloat16)
        pre_act = jnp.dot(normed_two, w_up, preferred_element_type=jnp.float32)
        act_vals, gelu_pull = jax.vjp(gelu_tanh, pre_act)
        hidden = act_vals.astype(jnp.bfloat16)
        part_two = jnp.dot(hidden, w_down, preferred_element_type=jnp.float32).astype(jnp.bfloat16)
        sum_two = lax.psum(part_two, "model")
        layer_out = (resid_rows.astype(jnp.float32) + sum_two.astype(jnp.float32)).astype(jnp.bfloat16)

        d_hidden = jnp.einsum("se,fe->sf", grad_y, w_down, preferred_element_type=jnp.float32).astype(jnp.bfloat16)
        d_down = jnp.einsum("sf,se->fe", hidden, grad_y, preferred_element_type=jnp.float32).astype(jnp.bfloat16)
        d_pre = gelu_pull(d_hidden.astype(jnp.float32))[0].astype(jnp.bfloat16)
        d_up = jnp.einsum("sh,sf->hf", normed_two, d_pre, preferred_element_type=jnp.float32).astype(jnp.bfloat16)
        part_three = jnp.einsum("sf,hf->sh", d_pre, w_up, preferred_element_type=jnp.float32).astype(jnp.bfloat16)
        d_normed_two = lax.psum(part_three, "model").astype(jnp.float32)
        d_in_two, d_gain_two = norm_backward(d_normed_two, hat_two, inv_two, gain_two)
        d_resid = (grad_y.astype(jnp.float32) + d_in_two).astype(jnp.bfloat16)
        d_wout = jnp.einsum("shd,se->hde", attn_rows, d_resid, preferred_element_type=jnp.float32).astype(jnp.bfloat16)
        d_attn = jnp.einsum("se,hde->shd", d_resid, w_out, preferred_element_type=jnp.float32).astype(jnp.bfloat16)
        d_query, d_key, d_value = attention_bwd(d_attn, q_rows, k_rows, v_rows, prob_f32, prob_bf)
        d_qkv = jnp.stack([d_query, d_key, d_value], axis=2).reshape(tokens, 3 * local_heads * head_dim)
        d_wqkv = jnp.einsum("sh,sc->hc", normed_one, d_qkv, preferred_element_type=jnp.float32).astype(jnp.bfloat16)
        part_four = jnp.einsum("sc,hc->sh", d_qkv, w_qkv, preferred_element_type=jnp.float32).astype(jnp.bfloat16)
        d_normed_one = lax.psum(part_four, "model").astype(jnp.float32)
        d_in_one, d_gain_one = norm_backward(d_normed_one, hat_one, inv_one, gain_one)
        grad_x = (d_resid.astype(jnp.float32) + d_in_one).astype(jnp.bfloat16)
        return (layer_out, grad_x, d_wqkv, d_wout, d_up, d_down,
                d_gain_one.astype(jnp.bfloat16), d_gain_two.astype(jnp.bfloat16))

    in_specs = (P("data", None), P("data"), P(None), P(None), P(None, "model"),
                P("model", None, None), P(None, "model"), P("model", None), P("data", None))
    out_specs = (P("data", None), P("data", None), P("data", "model"), P(("data", "model"), None, None),
                 P("data", "model"), P(("data", "model"), None), P("data"), P("data"))
    return jax.shard_map(local_layer, mesh=mesh, in_specs=in_specs, out_specs=out_specs, check_vma=False)
```

profile of v0, /device:TPU:0, one launch (start us, length us, event | category | flops | bytes accessed | tf_op | source)
XLA Modules:
  0.0 1445.3 jit_solution(6341694592259410197)
XLA Ops:
  23.9 42.5 %convolution_convert_fusion.8 = bf16[1536,1920]{1,0:T(8,128)(2,1)} fusion(bf16[5120,1920]{1,0:T(8,128)(2,1)} %param.13, bf16[1536,5120]{1,0:T(8,128)(2,1)} %param.9, f32[5120]{0:T(1024)S(1)} %convert_element_type.137, f32[1536]{0:T(1024)S(1)} %add_rsqrt_fusion.1, f32[1536]{0:T(1024)S(1)} %broadcast_multiply_fusion.5), kind=kOutput, calls=%fused_computation.94 | convolution fusion | flops 30241259520 | bytes 41320448 | tf_op jit(solution)/shard_map/dot_general | solution.py:61
  77.3 27.3 %fusion.100 = (f32[5,1536]{1,0:T(8,128)S(1)}, f32[5,1536,1536]{1,2,0:T(8,128)}) fusion(pred[1536,1536]{0,1:T(8,128)(4,1)S(1)} %fusion.62, bf16[1536,5,3,128]{0,3,2,1:T(8,128)(2,1)} %bitcast.78), kind=kOutput, calls=%fused_computation.125 | convolution fusion | flops 3067086336 | bytes 53508096 | tf_op jit(solution)/shard_map/sub | solution.py:34
  104.6 16.5 %fusion.84 = bf16[1536,5,128]{0,2,1:T(8,128)(2,1)S(1)} fusion(bf16[1536,5,3,128]{0,3,2,1:T(8,128)(2,1)} %bitcast.79, f32[5,1536,1536]{1,2,0:T(8,128)} %get-tuple-element.19, f32[5,1536]{1,0:T(8,128)S(1)} %get-tuple-element.18), kind=kOutput, calls=%fused_computation.105 | convolution fusion | flops 3044474880 | bytes 51148800 | tf_op jit(solution)/shard_map/hst,thd->shd/dot_general | solution.py:36
  122.5 18.1 %bitcast_convert_fusion = bf16[1536,5120]{1,0:T(8,128)(2,1)} fusion(bf16[1536,5,128]{0,2,1:T(8,128)(2,1)S(1)} %fusion.84, bf16[5,128,5120]{2,1,0:T(8,128)(2,1)} %param.14), kind=kOutput, calls=%fused_computation.53 | convolution fusion | flops 10074193920 | bytes 24248320 | tf_op jit(solution)/shard_map/shd,hde->se/dot_general | solution.py:67
  141.3 197.0 %all-reduce.5.cloned.1.call-done = bf16[1536,5120]{1,0:T(8,128)(2,1)} async-done(((bf16[1536,5120]{1,0:T(8,128)(2,1)}), bf16[1536,5120]{1,0:T(8,128)(2,1)}) %all-reduce.5.cloned.1.call-update) | async-done | bytes 15728656 | tf_op jit(solution)/shard_map/psum | solution.py:68
  363.8 51.6 %fusion.95 = f32[1536,2560]{1,0:T(8,128)} fusion(bf16[5120,2560]{1,0:T(8,128)(2,1)} %param.15, bf16[1536,5120]{1,0:T(8,128)(2,1)} %copy-done.2, f32[5120]{0:T(1024)S(1)} %convert_element_type.147, f32[1536]{0:T(1024)S(1)} %add_rsqrt_fusion, f32[1536]{0:T(1024)S(1)} %broadcast_multiply_fusion.4), kind=kOutput, calls=%fused_computation.124 | convolution fusion | flops 40304640000 | bytes 57704448 | tf_op jit(solution)/shard_map/dot_general | solution.py:72
  415.4 53.7 %convolution_convert_fusion = bf16[2560,5120]{1,0:T(8,128)(2,1)} fusion(bf16[1536,5120]{1,0:T(8,128)(2,1)} %param.17, f32[1536,2560]{1,0:T(8,128)} %fusion.95), kind=kOutput, calls=%fused_computation.54 | convolution fusion | flops 40313815040 | bytes 57671680 | tf_op jit(solution)/shard_map/sf,se->fe/dot_general | solution.py:80
  469.1 60.6 %fusion.44 = bf16[1536,2560]{1,0:T(8,128)(2,1)} fusion(f32[1536,2560]{1,0:T(8,128)} %fusion.95, bf16[1536,5120]{1,0:T(8,128)(2,1)} %param.17, bf16[2560,5120]{1,0:T(8,128)(2,1)} %param.16), kind=kOutput, calls=%fused_computation.71 | convolution fusion | flops 40351825920 | bytes 65536000 | tf_op jit(solution)/shard_map/se,fe->sf/dot_general | solution.py:79
  529.7 48.6 %convolution_convert_fusion.5 = bf16[1536,5120]{1,0:T(8,128)(2,1)} fusion(bf16[1536,2560]{1,0:T(8,128)(2,1)} %fusion.44, bf16[5120,2560]{1,0:T(8,128)(2,1)} %param.15), kind=kOutput, calls=%fused_computation.67 | convolution fusion | flops 40273182720 | bytes 49807360 | tf_op jit(solution)/shard_map/sf,hf->sh/dot_general | solution.py:83
  578.4 59.5 %convolution_convert_fusion.6 = bf16[1536,5120]{1,0:T(8,128)(2,1)} fusion(bf16[2560,5120]{1,0:T(8,128)(2,1)} %param.16, f32[1536,2560]{1,0:T(8,128)} %fusion.95), kind=kOutput, calls=%fused_computation.68 | convolution fusion | flops 40308572160 | bytes 57671680 | tf_op jit(solution)/shard_map/dot_general | solution.py:75
  637.9 135.5 %all-reduce.7.cloned.1.call-done = bf16[1536,5120]{1,0:T(8,128)(2,1)} async-done(((bf16[1536,5120]{1,0:T(8,128)(2,1)}), bf16[1536,5120]{1,0:T(8,128)(2,1)}) %all-reduce.7.cloned.1.call-update) | async-done | bytes 15728656 | tf_op jit(solution)/shard_map/psum | solution.py:84
  773.4 20.8 %fusion.34 = (bf16[5120]{0:T(1024)(128)(2,1)}, f32[1536]{0:T(1024)S(1)}, f32[1536]{0:T(1024)S(1)}) fusion(bf16[1536,5120]{1,0:T(8,128)(2,1)} %copy-done.2, bf16[1536,5120]{1,0:T(8,128)(2,1)} %all-reduce.7.cloned.1.call-done, f32[1536]{0:T(1024)S(1)} %copy-done.21, f32[1536]{0:T(1024)S(1)} %copy-done.16, f32[5120]{0:T(1024)S(1)} %copy-done.11), kind=kLoop, calls=%fused_computation.48 | loop fusion | flops 78635008 | bytes 31512576 | tf_op jit(solution)/shard_map/reduce_sum | solution.py:19
  794.2 32.3 %fusion.25 = bf16[1536,5120]{1,0:T(8,128)(2,1)} fusion(bf16[1536,5120]{1,0:T(8,128)(2,1)S(1)} %copy-done.3, bf16[1536,5120]{1,0:T(8,128)(2,1)S(1)} %copy-done.5, bf16[1536,5120]{1,0:T(8,128)(2,1)} %param.17, f32[1536]{0:T(1024)S(1)} %get-tuple-element.20, f32[1536]{0:T(1024)S(1)} %get-tuple-element.21, f32[5120]{0:T(1024)S(1)} %copy-done.11, ...), kind=kLoop, calls=%fused_computation.39 | loop fusion | flops 94371840 | bytes 62959616 | tf_op jit(solution)/shard_map/convert_element_type | solution.py:86
  826.6 17.2 %fusion.76 = bf16[1536,5,128]{2,0,1:T(8,128)(2,1)S(1)} fusion(bf16[5,128,5120]{2,1,0:T(8,128)(2,1)} %param.14, bf16[1536,5120]{1,0:T(8,128)(2,1)} %fusion.25), kind=kOutput, calls=%fused_computation.101 | convolution fusion | flops 10067312640 | bytes 24248320 | tf_op jit(solution)/shard_map/se,hde->shd/dot_general | solution.py:88
  843.8 18.9 %fusion.81 = bf16[1536,5,1,128]{0,3,1,2:T(8,128)(2,1)} fusion(bf16[1536,5,128]{2,0,1:T(8,128)(2,1)S(1)} %fusion.76, f32[5,1536,1536]{1,2,0:T(8,128)} %get-tuple-element.19, f32[5,1536]{1,0:T(8,128)S(1)} %copy-done.28), kind=kOutput, calls=%fused_computation.104 | convolution fusion | flops 3044474880 | bytes 51148800 | tf_op jit(solution)/shard_map/hst,shd->thd/dot_general | solution.py:48
  875.9 47.0 %fusion.79 = bf16[1536,5,1,128]{0,3,1,2:T(8,128)(2,1)} fusion(bf16[5,1536,1536]{1,2,0:T(8,128)(2,1)} %convolution_convert_fusion.2, bf16[1536,5,3,128]{0,3,2,1:T(8,128)(2,1)} %bitcast.81, f32[5,1536,1536]{1,2,0:T(8,128)} %get-tuple-element.19, f32[5,1536]{1,0:T(8,128)S(1)} %copy-done.28), kind=kOutput, calls=%fused_computation.102 | convolution fusion | flops 3127059456 | bytes 145588224 | tf_op jit(solution)/shard_map/hst,shd->thd/dot_general | solution.py:47
  923.0 46.9 %fusion.80 = bf16[1536,5,1,128]{0,3,1,2:T(8,128)(2,1)} fusion(bf16[5,1536,1536]{1,2,0:T(8,128)(2,1)} %convolution_convert_fusion.2, bf16[1536,5,3,128]{0,3,2,1:T(8,128)(2,1)} %bitcast.82, f32[5,1536,1536]{1,2,0:T(8,128)} %get-tuple-element.19, f32[5,1536]{1,0:T(8,128)S(1)} %copy-done.28), kind=kOutput, calls=%fused_computation.103 | convolution fusion | flops 3127059456 | bytes 145588224 | tf_op jit(solution)/shard_map/hst,thd->shd/dot_general | solution.py:46
  976.0 38.1 %convolution_convert_fusion.3 = bf16[1536,5120]{1,0:T(8,128)(2,1)} fusion(bf16[1536,1920]{0,1:T(8,128)(2,1)S(1)} %bitcast.83, bf16[5120,1920]{1,0:T(8,128)(2,1)} %param.13), kind=kOutput, calls=%fused_computation.65 | convolution fusion | flops 30206853120 | bytes 41287680 | tf_op jit(solution)/shard_map/sc,hc->sh/dot_general | solution.py:92
  1014.8 50.3 %convolution_convert_fusion.1 = bf16[5120,2560]{1,0:T(8,128)(2,1)} fusion(bf16[1536,2560]{1,0:T(8,128)(2,1)} %fusion.44, bf16[1536,5120]{1,0:T(8,128)(2,1)} %copy-done.2, f32[5120]{0:T(1024)S(1)} %copy-done.12, f32[1536]{0:T(1024)S(1)} %copy-done.22, f32[1536]{0:T(1024)S(1)} %copy-done.17), kind=kOutput, calls=%fused_computation.55 | convolution fusion | flops 40317747200 | bytes 49840128 | tf_op jit(solution)/shard_map/sh,sf->hf/dot_general | solution.py:82
  1077.6 42.2 %convolution_convert_fusion.4 = bf16[5120,1920]{1,0:T(8,128)(2,1)} fusion(bf16[1536,1920]{0,1:T(8,128)(2,1)} %bitcast.84, bf16[1536,5120]{1,0:T(8,128)(2,1)} %param.9, f32[5120]{0:T(1024)S(1)} %copy-done.9, f32[1536]{0:T(1024)S(1)} %copy-done.19, f32[1536]{0:T(1024)S(1)} %copy-done.14), kind=kOutput, calls=%fused_computation.66 | convolution fusion | flops 30248140800 | bytes 41320448 | tf_op jit(solution)/shard_map/sh,sc->hc/dot_general | solution.py:91
  1119.9 257.8 %all-reduce.9.cloned.1.call-done = (bf16[1536,5120]{1,0:T(8,128)(2,1)}, bf16[1536,5120]{1,0:T(8,128)(2,1)}) async-done(((bf16[1536,5120]{1,0:T(8,128)(2,1)}, bf16[1536,5120]{1,0:T(8,128)(2,1)}), (bf16[1536,5120]{1,0:T(8,128)(2,1)}, bf16[1536,5120]{1,0:T(8,128)(2,1)})) %all-reduce.9.cloned.1.call-update) | async-done | bytes 31457296 | tf_op jit(solution)/shard_map/psum | solution.py:76
  1377.7 20.8 %fusion.38 = bf16[1536,5120]{1,0:T(8,128)(2,1)} fusion(bf16[1536,5120]{1,0:T(8,128)(2,1)} %copy-done.2, bf16[1536,5120]{1,0:T(8,128)(2,1)} %get-tuple-element.14), kind=kLoop, calls=%fused_computation.52 | loop fusion | flops 31457280 | bytes 47185920 | tf_op jit(solution)/shard_map/convert_element_type | solution.py:77
  1402.5 15.7 %fusion.36 = (bf16[5120]{0:T(1024)(128)(2,1)}, f32[1536]{0:T(1024)S(1)}, f32[1536]{0:T(1024)S(1)}) fusion(bf16[1536,5120]{1,0:T(8,128)(2,1)S(1)} %copy-done.1, bf16[1536,5120]{1,0:T(8,128)(2,1)S(1)} %copy-done.4, f32[1536]{0:T(1024)S(1)} %copy-done.19, f32[1536]{0:T(1024)S(1)} %copy-done.14, f32[5120]{0:T(1024)S(1)} %copy-done.9), kind=kLoop, calls=%fused_computation.50 | loop fusion | flops 78635008 | bytes 31512576 | tf_op jit(solution)/shard_map/reduce_sum | solution.py:19
  1418.2 20.4 %fusion.31 = bf16[1536,5120]{1,0:T(8,128)(2,1)} fusion(bf16[1536,5120]{1,0:T(8,128)(2,1)S(1)} %copy-done.1, bf16[1536,5120]{1,0:T(8,128)(2,1)S(1)} %copy-done.4, bf16[1536,5120]{1,0:T(8,128)(2,1)} %fusion.25, f32[1536]{0:T(1024)S(1)} %broadcast_multiply_fusion, f32[1536]{0:T(1024)S(1)} %broadcast_multiply_fusion.1, f32[5120]{0:T(1024)S(1)} %copy-done.9, ...), kind=kLoop, calls=%fused_computation.45 | loop fusion | flops 94371840 | bytes 62959616 | tf_op jit(solution)/shard_map/convert_element_type | solution.py:95
  (92 shorter events, 91.6 us)
Async XLA Ops:
  7.2 331.1 %all-reduce.5.cloned.1.call-start = ((), (), s32[]{:S(2)}) async-start(), calls=%async_computation | async-start | bytes 31457280 | tf_op jit(solution)/shard_map/psum | solution.py:68
  8.1 15.2 %copy-start.8 = (f32[5120]{0:T(1024)}, f32[5120]{0:T(1024)S(1)}, u32[]{:S(2)}) copy-start(f32[5120]{0:T(1024)S(1)} %convert_element_type.137) | copy-start | bytes 61444
  23.9 51.0 %copy-start.23 = (s32[1536]{0:T(1024)S(1)}, s32[1536]{0:T(1024)}, u32[]{:S(2)}) copy-start(s32[1536]{0:T(1024)} %param.10) | copy-start | bytes 18436
  104.6 16.5 %copy-start.27 = (f32[5,1536]{1,0:T(8,128)}, f32[5,1536]{1,0:T(8,128)S(1)}, u32[]{:S(2)}) copy-start(f32[5,1536]{1,0:T(8,128)S(1)} %get-tuple-element.18) | copy-start | bytes 92164
  140.6 632.7 %all-reduce.7.cloned.1.call-start = ((), (), s32[]{:S(2)}) async-start(), calls=%async_computation.1 | async-start | bytes 31457280 | tf_op jit(solution)/shard_map/psum | solution.py:84
  141.3 222.5 %copy-start.10 = (f32[5120]{0:T(1024)}, f32[5120]{0:T(1024)S(1)}, u32[]{:S(2)}) copy-start(f32[5120]{0:T(1024)S(1)} %convert_element_type.147) | copy-start | bytes 61444
  352.1 63.4 %copy-start.15 = (f32[1536]{0:T(1024)}, f32[1536]{0:T(1024)S(1)}, u32[]{:S(2)}) copy-start(f32[1536]{0:T(1024)S(1)} %broadcast_multiply_fusion.4) | copy-start | bytes 18436
  363.8 51.7 %copy-start.20 = (f32[1536]{0:T(1024)}, f32[1536]{0:T(1024)S(1)}, u32[]{:S(2)}) copy-start(f32[1536]{0:T(1024)S(1)} %add_rsqrt_fusion) | copy-start | bytes 18436
  578.4 195.0 %copy-start.11 = (f32[5120]{0:T(1024)S(1)}, f32[5120]{0:T(1024)}, u32[]{:S(2)}) copy-start(f32[5120]{0:T(1024)} %copy-done.10) | copy-start | bytes 61444
  578.4 195.0 %copy-start.16 = (f32[1536]{0:T(1024)S(1)}, f32[1536]{0:T(1024)}, u32[]{:S(2)}) copy-start(f32[1536]{0:T(1024)} %copy-done.15) | copy-start | bytes 18436
  578.4 195.0 %copy-start.21 = (f32[1536]{0:T(1024)S(1)}, f32[1536]{0:T(1024)}, u32[]{:S(2)}) copy-start(f32[1536]{0:T(1024)} %copy-done.20) | copy-start | bytes 18436
  578.4 799.3 %all-reduce.9.cloned.1.call-start = ((), (), s32[]{:S(2)}) async-start(), calls=%async_computation.2 | async-start | bytes 62914560 | tf_op jit(solution)/shard_map/psum | solution.py:76
  773.4 20.8 %copy-start.3 = (bf16[1536,5120]{1,0:T(8,128)(2,1)S(1)}, bf16[1536,5120]{1,0:T(8,128)(2,1)}, u32[]{:S(2)}) copy-start(bf16[1536,5120]{1,0:T(8,128)(2,1)} %copy-done.2) | copy-start | bytes 47185924
  773.4 20.8 %copy-start.5 = (bf16[1536,5120]{1,0:T(8,128)(2,1)S(1)}, bf16[1536,5120]{1,0:T(8,128)(2,1)}, u32[]{:S(2)}) copy-start(bf16[1536,5120]{1,0:T(8,128)(2,1)} %all-reduce.7.cloned.1.call-done) | copy-start | bytes 47185924
  826.6 17.2 %copy-start.28 = (f32[5,1536]{1,0:T(8,128)S(1)}, f32[5,1536]{1,0:T(8,128)}, u32[]{:S(2)}) copy-start(f32[5,1536]{1,0:T(8,128)} %copy-done.27) | copy-start | bytes 92164
  923.0 46.9 %copy-start.7 = (bf16[1536,5,1,128]{0,3,1,2:T(8,128)(2,1)S(1)}, bf16[1536,5,1,128]{0,3,1,2:T(8,128)(2,1)}, u32[]{:S(2)}) copy-start(bf16[1536,5,1,128]{0,3,1,2:T(8,128)(2,1)} %fusion.81) | copy-start | bytes 5898244
  1014.1 51.1 %slice-start = ((s8[15728640]{0:T(1024)(128)(4,1)}), s8[3145728]{0:T(1024)(128)(4,1)S(1)}, s32[]{:S(2)}) async-start(s8[15728640]{0:T(1024)(128)(4,1)} %bitcast.76), calls=%async_computation.3 | async-start | bytes 6291456
  1014.8 50.4 %slice-start.1 = ((s8[15728640]{0:T(1024)(128)(4,1)}), s8[4194304]{0:T(1024)(128)(4,1)S(1)}, s32[]{:S(2)}) async-start(s8[15728640]{0:T(1024)(128)(4,1)} %bitcast.76), calls=%async_computation.4 | async-start | bytes 8388608
  1014.8 50.4 %slice-start.2 = ((s8[15728640]{0:T(1024)(128)(4,1)}), s8[4194304]{0:T(1024)(128)(4,1)S(1)}, s32[]{:S(2)}) async-start(s8[15728640]{0:T(1024)(128)(4,1)} %bitcast.76), calls=%async_computation.5 | async-start | bytes 8388608
  1014.8 50.4 %slice-start.3 = ((s8[15728640]{0:T(1024)(128)(4,1)}), s8[4194304]{0:T(1024)(128)(4,1)S(1)}, s32[]{:S(2)}) async-start(s8[15728640]{0:T(1024)(128)(4,1)} %bitcast.76), calls=%async_computation.6 | async-start | bytes 8388608
  1014.8 50.4 %copy-start.26 = (bf16[1536,5,128]{0,2,1:T(8,128)(2,1)S(1)}, bf16[1536,5,128]{0,2,1:T(8,128)(2,1)}, u32[]{:S(2)}) copy-start(bf16[1536,5,128]{0,2,1:T(8,128)(2,1)} %copy-done.25) | copy-start | bytes 5898244
  1065.2 12.4 copy-start.9
  1377.7 20.8 %copy-start.1 = (bf16[1536,5120]{1,0:T(8,128)(2,1)S(1)}, bf16[1536,5120]{1,0:T(8,128)(2,1)}, u32[]{:S(2)}) copy-start(bf16[1536,5120]{1,0:T(8,128)(2,1)} %param.9) | copy-start | bytes 47185924
  1377.7 24.8 %copy-start.4 = (bf16[1536,5120]{1,0:T(8,128)(2,1)S(1)}, bf16[1536,5120]{1,0:T(8,128)(2,1)}, u32[]{:S(2)}) copy-start(bf16[1536,5120]{1,0:T(8,128)(2,1)} %get-tuple-element.15) | copy-start | bytes 47185924
  (12 other events, 54.1 us)
Sparse Core Ops, SparseCore 0:
  140.7 197.5 all-reduce.4
  578.5 194.8 all-reduce.6
  1014.2 363.3 all-reduce.8
where the time goes:
time: 1450 us
  matrix products  665 us (46%)
  waiting for transfers between devices  590 us (41%)
  other arithmetic  149 us (10%)
  local copies, waits for them, and re-layouts  27 us (2%)
    psum x1, waiting for transfers between devices, local_layer(): sum_two = lax.psum(part_two, 'model')  258 us
    psum x1, waiting for transfers between devices, local_layer(): sum_one = lax.psum(part_one, 'model')  197 us
    psum x1, waiting for transfers between devices, local_layer(): d_normed_two = lax.psum(part_three, 'model').astype(jnp.float32)  135 us
    dot_general x1, matrix products, local_layer(): jnp.einsum('se,fe->sf', grad_y, w_down, preferred_element_type=jnp.float32)  60.6 us
    dot_general x1, matrix products, local_layer(): jnp.dot(hidden, w_down, preferred_element_type=jnp.float32)  59.5 us
    dot_general x1, matrix products, local_layer(): jnp.einsum('sf,se->fe', hidden, grad_y, preferred_element_type=jnp.float32)  53.7 us
    dot_general x1, matrix products, local_layer(): pre_act = jnp.dot(normed_two, w_up, preferred_element_type=jnp.float32)  51.6 us
    dot_general x1, matrix products, local_layer(): jnp.einsum('sh,sf->hf', normed_two, d_pre, preferred_element_type=jnp.flo...  50.3 us
  transfers between devices with their start and end apart: 3, of which 3 were waited for; matrix products, arithmetic and copies ran while one was open for 11% of the time, Pallas kernels for 0%

commit v1 on v0

v1 whole, which is shorter than its diff:
```python
import functools
import jax
import jax.numpy as jnp
from jax import lax
from jax.experimental import pallas as pl
from jax.experimental.pallas import tpu as pltpu
from jax.sharding import PartitionSpec as P

LN_EPS = 1e-5
TILE = 256
BF = jnp.bfloat16
F32 = jnp.float32
gelu_tanh = functools.partial(jax.nn.gelu, approximate=True)


def mm(spec, left, right):
    return jnp.einsum(spec, left, right, preferred_element_type=F32)


def normalize(values):
    values_f32 = values.astype(F32)
    centered = values_f32 - jnp.mean(values_f32, axis=-1, keepdims=True)
    inv_std = lax.rsqrt(jnp.mean(centered * centered, axis=-1, keepdims=True) + LN_EPS)
    return centered * inv_std, inv_std


def norm_backward(grad_out, x_hat, inv_std, gain_vec):
    d_gain = jnp.sum(grad_out * x_hat, axis=0)
    d_hat = grad_out * gain_vec.astype(F32)
    d_in = inv_std * (d_hat - jnp.mean(d_hat, axis=-1, keepdims=True)
                      - x_hat * jnp.mean(d_hat * x_hat, axis=-1, keepdims=True))
    return d_in, d_gain


def dot_nt(left, right):
    return lax.dot_general(left, right, (((1,), (1,)), ((), ())), preferred_element_type=F32)


def dot_tn(left, right):
    return lax.dot_general(left, right, (((0,), (0,)), ((), ())), preferred_element_type=F32)


def dot_nn(left, right):
    return lax.dot_general(left, right, (((1,), (0,)), ((), ())), preferred_element_type=F32)


def scores_t(keys, query, segk_ref, segq, k_start, diagonal):
    block = dot_nt(keys, query) * (query.shape[-1] ** -0.5)
    seen = segk_ref[k_start:k_start + TILE, :] == segq
    if diagonal:
        seen = seen & (lax.broadcasted_iota(jnp.int32, (TILE, TILE), 0)
                       <= lax.broadcasted_iota(jnp.int32, (TILE, TILE), 1))
    return jnp.where(seen, block, -1e30)


def key_blocks(prev, cur, rows, tile, first, dim, part):
    out = []
    for c, ref in enumerate(prev):
        out += [(ref, r, c * rows + r) for r in range(0, rows, TILE)]
    out += [(cur, r, first + r) for r in range(0, (tile + 1) * TILE, TILE)]
    return out


def attn_fwd_kernel(n_prev, rows, dim, *refs):
    segk_ref, segq_ref = refs[:2]
    prev, cur = refs[2:2 + n_prev], refs[2 + n_prev]
    o_ref, stat_ref, s_ref, p_ref = refs[3 + n_prev:]
    first = n_prev * rows
    for t in range(rows // TILE):
        lo = t * TILE
        query = cur[lo:lo + TILE, 0:dim]
        segq = segq_ref[:, first + lo:first + lo + TILE]
        blocks = key_blocks(prev, cur, rows, t, first, dim, 1)
        top = None
        for n, (ref, r, start) in enumerate(blocks):
            block = scores_t(ref[r:r + TILE, dim:2 * dim], query, segk_ref, segq, start, n == len(blocks) - 1)
            s_ref[n * TILE:(n + 1) * TILE, :] = block
            here = jnp.max(block, axis=0, keepdims=True)
            top = here if top is None else jnp.maximum(top, here)
        total = None
        for n in range(len(blocks)):
            expd = jnp.exp(s_ref[n * TILE:(n + 1) * TILE, :] - top)
            s_ref[n * TILE:(n + 1) * TILE, :] = expd
            here = jnp.sum(expd, axis=0, keepdims=True)
            total = here if total is None else total + here
        inv = 1.0 / total
        for n in range(len(blocks)):
            p_ref[n * TILE:(n + 1) * TILE, :] = (s_ref[n * TILE:(n + 1) * TILE, :] * inv).astype(BF)
        out_t = dot_tn(cur[0:lo + TILE, 2 * dim:3 * dim], p_ref[first:first + lo + TILE, :])
        for c, ref in enumerate(prev):
            out_t = out_t + dot_tn(ref[:, 2 * dim:3 * dim], p_ref[c * rows:(c + 1) * rows, :])
        o_ref[lo:lo + TILE, :] = out_t.T.astype(BF)
        stat_ref[0, 0:1, lo:lo + TILE] = top
        stat_ref[0, 1:2, lo:lo + TILE] = inv


def attn_bwd_kernel(n_prev, n_later, rows, dim, *refs):
    segk_ref, segq_ref = refs[:2]
    prev, cur = refs[2:2 + n_prev], refs[2 + n_prev]
    do_ref, stat_ref = refs[3 + n_prev:5 + n_prev]
    later = refs[5 + n_prev:5 + n_prev + n_later]
    rest = refs[5 + n_prev + n_later:]
    dqkv_ref, dkv_prev = rest[0], rest[1:1 + n_prev]
    p_ref, dp_ref, ds_ref, acc_k, acc_v = rest[1 + n_prev:]
    first = n_prev * rows
    scale = dim ** -0.5
    acc_k[...] = jnp.zeros_like(acc_k)
    acc_v[...] = jnp.zeros_like(acc_v)
    for ref in later:
        acc_k[first:first + rows, :] += ref[:, 0:dim]
        acc_v[first:first + rows, :] += ref[:, dim:2 * dim]
    for t in range(rows // TILE):
        lo = t * TILE
        query = cur[lo:lo + TILE, 0:dim]
        d_out = do_ref[lo:lo + TILE, :]
        segq = segq_ref[:, first + lo:first + lo + TILE]
        top = stat_ref[0, 0:1, lo:lo + TILE]
        inv = stat_ref[0, 1:2, lo:lo + TILE]
        blocks = key_blocks(prev, cur, rows, t, first, dim, 1)
        delta = jnp.zeros_like(top)
        for n, (ref, r, start) in enumerate(blocks):
            block = scores_t(ref[r:r + TILE, dim:2 * dim], query, segk_ref, segq, start, n == len(blocks) - 1)
            prob = jnp.exp(block - top) * inv
            d_prob = dot_nt(ref[r:r + TILE, 2 * dim:3 * dim], d_out).astype(BF)
            delta += jnp.sum(prob * d_prob.astype(F32), axis=0, keepdims=True)
            p_ref[n * TILE:(n + 1) * TILE, :] = prob
            dp_ref[n * TILE:(n + 1) * TILE, :] = d_prob
        for n in range(len(blocks)):
            span = slice(n * TILE, (n + 1) * TILE)
            prob = p_ref[span, :]
            d_score = (prob * (dp_ref[span, :].astype(F32) - delta) * scale).astype(BF)
            ds_ref[span, :] = d_score
            acc_v[span, :] += dot_nn(prob.astype(BF), d_out)
            acc_k[span, :] += dot_nn(d_score, query)
        dq_t = dot_tn(cur[0:lo + TILE, dim:2 * dim], ds_ref[first:first + lo + TILE, :])
        for c, ref in enumerate(prev):
            dq_t = dq_t + dot_tn(ref[:, dim:2 * dim], ds_ref[c * rows:(c + 1) * rows, :])
        dqkv_ref[lo:lo + TILE, 0:dim] = dq_t.T.astype(BF)
    dqkv_ref[:, dim:2 * dim] = acc_k[first:first + rows, :].astype(BF)
    dqkv_ref[:, 2 * dim:3 * dim] = acc_v[first:first + rows, :].astype(BF)
    for c, ref in enumerate(dkv_prev):
        ref[:, 0:dim] = acc_k[c * rows:(c + 1) * rows, :]
        ref[:, dim:2 * dim] = acc_v[c * rows:(c + 1) * rows, :]


def whole(shape):
    return pl.BlockSpec(shape, lambda h: (0,) * len(shape))


def by_head(rows, cols):
    return pl.BlockSpec((rows, cols), lambda h: (0, h))


def attn_cost(n_prev, rows, heads, dim, dots):
    area = rows * (n_prev * rows + rows // 2) * heads
    return pl.CostEstimate(flops=2 * area * dim * dots * 2, bytes_accessed=rows * heads * dim * 12, transcendentals=area)


def attention_fwd(segk, segq, qkv_prev, qkv_cur, heads, dim):
    rows, n_prev = qkv_cur.shape[0], len(qkv_prev)
    keys = (n_prev + 1) * rows
    return pl.pallas_call(
        functools.partial(attn_fwd_kernel, n_prev, rows, dim),
        grid=(heads,),
        in_specs=[whole(segk.shape), whole(segq.shape)] + [by_head(rows, 3 * dim)] * (n_prev + 1),
        out_specs=[by_head(rows, dim), pl.BlockSpec((1, 2, rows), lambda h: (h, 0, 0))],
        out_shape=[jax.ShapeDtypeStruct((rows, heads * dim), BF), jax.ShapeDtypeStruct((heads, 2, rows), F32)],
        scratch_shapes=[pltpu.VMEM((keys, TILE), F32), pltpu.VMEM((keys, TILE), BF)],
        cost_estimate=attn_cost(n_prev, rows, heads, dim, 2),
        name=f"attn_fwd_{n_prev}",
    )(segk, segq, *qkv_prev, qkv_cur)


def attention_bwd(segk, segq, qkv_prev, qkv_cur, d_out, stats, later, heads, dim):
    rows, n_prev = qkv_cur.shape[0], len(qkv_prev)
    keys = (n_prev + 1) * rows
    return pl.pallas_call(
        functools.partial(attn_bwd_kernel, n_prev, len(later), rows, dim),
        grid=(heads,),
        in_specs=[whole(segk.shape), whole(segq.shape)] + [by_head(rows, 3 * dim)] * (n_prev + 1)
        + [by_head(rows, dim), pl.BlockSpec((1, 2, rows), lambda h: (h, 0, 0))] + [by_head(rows, 2 * dim)] * len(later),
        out_specs=[by_head(rows, 3 * dim)] + [by_head(rows, 2 * dim)] * n_prev,
        out_shape=[jax.ShapeDtypeStruct((rows, 3 * heads * dim), BF)]
        + [jax.ShapeDtypeStruct((rows, 2 * heads * dim), F32)] * n_prev,
        scratch_shapes=[pltpu.VMEM((keys, TILE), F32), pltpu.VMEM((keys, TILE), BF), pltpu.VMEM((keys, TILE), BF),
                        pltpu.VMEM((keys, dim), F32), pltpu.VMEM((keys, dim), F32)],
        cost_estimate=attn_cost(n_prev, rows, heads, dim, 5),
        name=f"attn_bwd_{n_prev}",
    )(segk, segq, *qkv_prev, qkv_cur, d_out, stats, *later)


def wgrad_kernel(n, *refs):
    out = dot_tn(refs[0][...], refs[n][...])
    for c in range(1, n):
        out += dot_tn(refs[c][...], refs[n + c][...])
    refs[2 * n][...] = out.astype(BF)


def weight_grad(lefts, rights, tile_m, tile_n, name):
    n, rows = len(lefts), lefts[0].shape[0]
    rights = [r if isinstance(r, tuple) else (r, 0) for r in rights]
    m_dim, n_dim = lefts[0].shape[1], rights[0][0].shape[1]
    in_specs = [pl.BlockSpec((rows, tile_m), lambda i, j: (0, i)) for _ in lefts]
    in_specs += [pl.BlockSpec((rows, tile_n), functools.partial(lambda b, i, j: (b, j), b)) for _, b in rights]
    return pl.pallas_call(
        functools.partial(wgrad_kernel, n),
        grid=(m_dim // tile_m, n_dim // tile_n),
        in_specs=in_specs,
        out_specs=pl.BlockSpec((tile_m, tile_n), lambda i, j: (i, j)),
        out_shape=jax.ShapeDtypeStruct((m_dim, n_dim), BF),
        cost_estimate=pl.CostEstimate(flops=2 * n * rows * m_dim * n_dim, transcendentals=0,
                                      bytes_accessed=2 * (n * rows * (m_dim + n_dim) + m_dim * n_dim)),
        compiler_params=pltpu.CompilerParams(vmem_limit_bytes=56 * 1024 * 1024),
        name=name,
    )(*lefts, *[r for r, _ in rights])


def ln_fwd_kernel(x_ref, gain_ref, o_ref):
    hat, _ = normalize(x_ref[...])
    o_ref[...] = (hat * gain_ref[...].astype(F32)).astype(BF)


def ln_mid_kernel(x_ref, sum_ref, gain_ref, x1_ref, o_ref):
    resid = (x_ref[...].astype(F32) + sum_ref[...].astype(F32)).astype(BF)
    x1_ref[...] = resid
    hat, _ = normalize(resid)
    o_ref[...] = (hat * gain_ref[...].astype(F32)).astype(BF)


def ln_bwd_kernel(x_ref, d_ref, gain_ref, resid_ref, o_ref, dg_ref):
    hat, inv_std = normalize(x_ref[...])
    d_in, d_gain = norm_backward(d_ref[...].astype(F32), hat, inv_std, gain_ref[...])
    o_ref[...] = (resid_ref[...].astype(F32) + d_in).astype(BF)
    dg_ref[...] = d_gain[None, :]


def add_kernel(x_ref, sum_ref, o_ref):
    o_ref[...] = (x_ref[...].astype(F32) + sum_ref[...].astype(F32)).astype(BF)


def row_call(kernel, arrays, outs, name, tile=None, start=0):
    rows, width = outs[0][0], arrays[0].shape[1]
    tile = tile or rows
    spec = lambda r, s=0: pl.BlockSpec((r if r == 1 else tile, width), (lambda i: (0, 0)) if r == 1 else (lambda i: (i + s, 0)))
    return pl.pallas_call(
        kernel,
        grid=(rows // tile,),
        in_specs=[spec(a.shape[0], start) for a in arrays],
        out_specs=[spec(r) for r, _ in outs],
        out_shape=[jax.ShapeDtypeStruct((r, width), d) for r, d in outs],
        cost_estimate=pl.CostEstimate(flops=20 * rows * width, bytes_accessed=8 * rows * width, transcendentals=0),
        name=name,
    )(*arrays)


def after(value, *deps):
    return lax.optimization_barrier((value, *deps))[0]


N_CHUNKS = 2


def solution(mesh):
    n_dev = mesh.shape["model"]

    def local_layer(act_x, seg_ids, gain_one, gain_two, w_qkv, w_out, w_up, w_down, grad_y):
        tokens, width = act_x.shape
        heads, dim = w_out.shape[0], w_out.shape[1]
        w_proj = w_out.reshape(heads * dim, width)
        rows = tokens // N_CHUNKS
        own = rows // n_dev
        me = lax.axis_index("model")
        chunks = range(N_CHUNKS)

        def own_rows(array, c):
            return lax.dynamic_slice(array, (c * rows + me * own, 0), (own, array.shape[1]))

        def chunk_of(array, c):
            return array[c * rows:(c + 1) * rows]

        def reduce_rows(part):
            return lax.psum_scatter(part, "model", scatter_dimension=0, tiled=True)

        def gather_rows(block):
            return lax.all_gather(block, "model", axis=0, tiled=True)

        segk = jnp.broadcast_to(seg_ids[:, None], (tokens, TILE))
        segq = seg_ids[None, :]
        gain_one, gain_two = gain_one[None, :], gain_two[None, :]
        last = [seg_ids]

        def turn(value, *deps):
            return after(value, last[0], *deps)

        def done(value):
            last[0] = value
            return value

        def norm_in(c):
            return done(row_call(ln_fwd_kernel, [turn(act_x), gain_one], [(rows, BF)], f"ln1_{c}", 128, c * rows // 128)[0])

        normed_one, qkv, attn, stats, x_own, x1_own, normed_two = [], [], [], [], [], [None] * N_CHUNKS, [None] * N_CHUNKS
        sum_one = []
        for c in chunks:
            normed_one.append(norm_in(c))
            qkv.append(done(mm("sh,hc->sc", turn(normed_one[c]), w_qkv).astype(BF)))
            out, stat = attention_fwd(segk, turn(segq), qkv[:c], qkv[c], heads, dim)
            attn.append(done(out))
            stats.append(stat)
            part = done(mm("sc,ce->se", turn(attn[c]), w_proj).astype(BF))
            sum_one.append(reduce_rows(part))
            x_own.append(own_rows(act_x, c))

        d_hidden = []
        for c in chunks:
            d_hidden.append(done(after(mm("se,fe->sf", chunk_of(turn(grad_y), c), w_down).astype(BF))))
            x1_own[c], block = row_call(ln_mid_kernel, [turn(x_own[c]), sum_one[c], gain_two], [(own, BF)] * 2, f"ln2_{c}")
            normed_two[c] = gather_rows(done(block))

        hidden, d_pre, sum_three = [], [], []
        for c in chunks:
            pre_act = mm("sh,hf->sf", turn(normed_two[c]), w_up)
            act_vals, gelu_pull = jax.vjp(gelu_tanh, pre_act)
            hidden.append(act_vals.astype(BF))
            d_pre.append(done(gelu_pull(d_hidden[c].astype(F32))[0].astype(BF)))
            sum_three.append(reduce_rows(done(mm("sf,hf->sh", turn(d_pre[c]), w_up).astype(BF))))

        part_two = [done(mm("sf,fe->se", turn(hidden[c]), w_down).astype(BF)) for c in chunks]
        d_down = done(weight_grad([turn(hidden[0]), hidden[1]], [(grad_y, c) for c in chunks], 1280, 1280, "d_down"))

        d_resid_own, d_resid, dg_two = [None] * N_CHUNKS, [None] * N_CHUNKS, [None] * N_CHUNKS
        for c in reversed(chunks):
            d_resid_own[c], dg_two[c] = row_call(
                ln_bwd_kernel, [turn(x1_own[c]), sum_three[c], gain_two, own_rows(grad_y, c)], [(own, BF), (1, F32)], f"ln2b_{c}")
            d_resid[c] = gather_rows(done(d_resid_own[c]))

        d_up = done(weight_grad([turn(normed_two[0]), normed_two[1]], d_pre, 1280, 1280, "d_up"))

        d_qkv, later, sum_four, sum_two = [None] * N_CHUNKS, [], [None] * N_CHUNKS, [None] * N_CHUNKS
        for c in reversed(chunks):
            d_attn = done(mm("se,ce->sc", turn(d_resid[c]), w_proj).astype(BF))
            sum_two[c] = reduce_rows(after(part_two[c], d_attn))
            outs = attention_bwd(segk, turn(segq), qkv[:c], qkv[c], d_attn, stats[c], later, heads, dim)
            d_qkv[c], later = done(outs[0]), outs[1:]
            sum_four[c] = reduce_rows(done(mm("sc,hc->sh", turn(d_qkv[c]), w_qkv).astype(BF)))

        y_chunks, x_chunks, dg_one = [None] * N_CHUNKS, [None] * N_CHUNKS, [None] * N_CHUNKS
        for c in reversed(chunks):
            y_own = done(row_call(add_kernel, [turn(x1_own[c]), sum_two[c]], [(own, BF)], f"y_{c}")[0])
            y_chunks[c] = gather_rows(y_own)
            if c == N_CHUNKS - 1:
                d_wout = done(weight_grad([turn(attn[0]), attn[1]], d_resid, heads * dim, 1280, "d_wout"))
            else:
                d_wqkv = done(weight_grad([turn(normed_one[0]), normed_one[1]], d_qkv, 1024, 3 * heads * dim, "d_wqkv"))
            x_new, dg_one[c] = row_call(
                ln_bwd_kernel, [turn(x_own[c]), sum_four[c], gain_one, d_resid_own[c]], [(own, BF), (1, F32)], f"ln1b_{c}")
            x_chunks[c] = gather_rows(done(x_new))

        layer_out = jnp.concatenate(y_chunks, axis=0)
        dg = lax.psum(jnp.concatenate([dg_one[0] + dg_one[1], dg_two[0] + dg_two[1]], axis=0), "model").astype(BF)
        grad_x = jnp.concatenate(x_chunks, axis=0)
        return layer_out, grad_x, d_wqkv, d_wout.reshape(heads, dim, width), d_up, d_down, dg[0], dg[1]

    in_specs = (P("data", None), P("data"), P(None), P(None), P(None, "model"),
                P("model", None, None), P(None, "model"), P("model", None), P("data", None))
    out_specs = (P("data", None), P("data", None), P("data", "model"), P(("data", "model"), None, None),
                 P("data", "model"), P(("data", "model"), None), P("data"), P("data"))
    return jax.shard_map(local_layer, mesh=mesh, in_specs=in_specs, out_specs=out_specs, check_vma=False)
```

time: 1450 us -> 1060 us (0.73)
  matrix products: 665 us -> 357 us
  Pallas kernels: 0 us -> 262 us
  waiting for transfers between devices: 590 us -> 350 us
  other arithmetic: 149 us -> 27.2 us
  blocking collectives: 0 us -> 22.9 us
    psum x3 -> x0, waiting for transfers between devices: 590 us -> none  [the longest x1 258 us: local_layer(): sum_two = lax.psum(part_two, 'model')]
    dot_general x17 -> x16, matrix products: 637 us -> 357 us  [mm(): return jnp.einsum(spec, left, right, preferred_element_type=F32)]
    pallas_call x0 -> x18, Pallas kernels: none -> 262 us  [the longest x4 150 us: weight_grad(): pl.pallas_call(functools.partial(wgrad_kernel, n), grid=(m_dim // tile_m,...]
    all_gather x0 -> x8, waiting for transfers between devices: none -> 196 us  [gather_rows(): return lax.all_gather(block, 'model', axis=0, tiled=True)]
    reduce_scatter x0 -> x8, waiting for transfers between devices: none -> 152 us  [reduce_rows(): return lax.psum_scatter(part, 'model', scatter_dimension=0, tiled=True)]
    convert_element_type x5 -> x0, other arithmetic: 74.4 us -> none  [the longest x1 32.3 us: local_layer(): d_resid = (grad_y.astype(jnp.float32) + d_in_two).astype(jnp.bfloat16)]
    reduce_sum x6 -> x0, other arithmetic: 69 us -> none  [the longest x2 36.5 us: norm_backward(): d_gain = jnp.sum(grad_out * x_hat, axis=0)]
    sub x1 -> x0, matrix products: 27.3 us -> none  [attention_fwd(): prob_f32 = jax.nn.softmax(scores, axis=-1)]
  transfers between devices with their start and end apart: 3 -> 16, of which waited for: 3 -> 11; matrix products, arithmetic and copies ran while one was open for 11% -> 27% of each run, Pallas kernels for 0% -> 23%
where the time goes in v1:
time: 1060 us; the launch traced here: 1050 us
  matrix products  357 us (34%)
  waiting for transfers between devices  350 us (33%)
  Pallas kernels  262 us (25%)
  other arithmetic  27.2 us (3%)
  blocking collectives  22.9 us (2%)
  local copies, waits for them, and re-layouts  15.2 us (1%)
  between operations  14.5 us (1%)
    dot_general x16, matrix products, mm(): return jnp.einsum(spec, left, right, preferred_element_type=F32)  357 us
    all_gather x8, waiting for transfers between devices, gather_rows(): return lax.all_gather(block, 'model', axis=0, tiled=True)  196 us
    reduce_scatter x8, waiting for transfers between devices, reduce_rows(): return lax.psum_scatter(part, 'model', scatter_dimension=0, tiled=True)  152 us
    pallas_call x4, Pallas kernels, weight_grad(): pl.pallas_call(functools.partial(wgrad_kernel, n), grid=(m_dim // tile_m,...  150 us
    pallas_call x10, Pallas kernels, row_call(): pl.pallas_call(kernel, grid=(rows // tile,), in_specs=[spec(a.shape[0], s...  53.8 us
    pallas_call x2, Pallas kernels, attention_bwd(): pl.pallas_call(functools.partial(attn_bwd_kernel, n_prev, len(later), row...  34.6 us
    pallas_call x2, Pallas kernels, attention_fwd(): pl.pallas_call(functools.partial(attn_fwd_kernel, n_prev, rows, dim), gri...  23.6 us
    psum x1, blocking collectives, local_layer(): lax.psum(jnp.concatenate([dg_one[0] + dg_one[1], dg_two[0] + dg_two[1]],...  22.9 us
  transfers between devices with their start and end apart: 16, of which 11 were waited for; matrix products, arithmetic and copies ran while one was open for 27% of the time, Pallas kernels for 23%

profile of v1, /device:TPU:0, one launch (start us, length us, event | category | flops | bytes accessed | tf_op | source)
XLA Modules:
  0.0 1050.3 jit_solution(2873814188417010502)
XLA Ops:
  20.5 22.6 %convolution_convert_fusion.9.refs_2_ = bf16[768,1920]{1,0:T(8,128)(2,1)} fusion(bf16[768,5120]{1,0:T(8,128)(2,1)} %ln1_0.1.refs_0_, bf16[5120,1920]{1,0:T(8,128)(2,1)} %param.13), kind=kOutput, calls=%fused_computation.47 | convolution fusion | flops 15100968960 | bytes 30474240 | tf_op jit(solution)/shard_map/sh,hc->sc/dot_general | solution.py:17
  75.4 22.6 %convolution_convert_fusion.8.refs_3_ = bf16[768,1920]{1,0:T(8,128)(2,1)} fusion(bf16[768,5120]{1,0:T(8,128)(2,1)} %ln1_1.1.refs_1_, bf16[5120,1920]{1,0:T(8,128)(2,1)} %param.13), kind=kOutput, calls=%fused_computation.46 | convolution fusion | flops 15100968960 | bytes 30474240 | tf_op jit(solution)/shard_map/sh,hc->sc/dot_general | solution.py:17
  123.4 27.0 %fusion.24 = bf16[768,2560]{1,0:T(8,128)(2,1)} fusion(bf16[2560,5120]{1,0:T(8,128)(2,1)} %param.16, bf16[1536,5120]{1,0:T(8,128)(2,1)} %refs_3_.1), kind=kOutput, calls=%fused_computation.44 | convolution fusion | flops 20134625280 | bytes 38010880 | tf_op jit(solution)/shard_map/se,fe->sf/dot_general | solution.py:17
  157.5 27.0 %fusion.27 = bf16[768,2560]{1,0:T(8,128)(2,1)} fusion(bf16[2560,5120]{1,0:T(8,128)(2,1)} %param.16, bf16[1536,5120]{1,0:T(8,128)(2,1)} %refs_3_.1), kind=kOutput, calls=%fused_computation.45 | convolution fusion | flops 20134625280 | bytes 38010880 | tf_op jit(solution)/shard_map/se,fe->sf/dot_general | solution.py:17
  195.7 44.9 %all-gather.9.cloned.1.call-done.refs_0_ = bf16[768,5120]{1,0:T(8,128)(2,1)} async-done(((bf16[96,5120]{1,0:T(8,128)(2,1)}), bf16[768,5120]{1,0:T(8,128)(2,1)}) %all-gather.9.cloned.1.call-update) | async-done | bytes 7864336 | tf_op jit(solution)/shard_map/all_gather | solution.py:285
  240.6 32.4 %fusion.2 = (bf16[768,2560]{1,0:T(8,128)(2,1)S(1)}, bf16[768,2560]{1,0:T(8,128)(2,1)}) fusion(bf16[768,2560]{1,0:T(8,128)(2,1)} %fusion.24, bf16[768,5120]{1,0:T(8,128)(2,1)} %all-gather.9.cloned.1.call-done.refs_0_, bf16[5120,2560]{1,0:T(8,128)(2,1)} %param.15), kind=kOutput, calls=%fused_computation.20 | convolution fusion | flops 20177879040 | bytes 45875200 | tf_op jit(solution)/shard_map/sh,hf->sf/dot_general | solution.py:17
  274.9 25.3 %convolution_convert_fusion.7 = bf16[768,5120]{1,0:T(8,128)(2,1)} fusion(bf16[768,2560]{1,0:T(8,128)(2,1)S(1)} %get-tuple-element.81.refs_2_, bf16[5120,2560]{1,0:T(8,128)(2,1)} %param.15), kind=kOutput, calls=%fused_computation.17 | convolution fusion | flops 20136591360 | bytes 38010880 | tf_op jit(solution)/shard_map/sf,hf->sh/dot_general | solution.py:17
  300.2 32.2 %fusion.7 = (bf16[768,2560]{1,0:T(8,128)(2,1)S(1)}, bf16[768,2560]{1,0:T(8,128)(2,1)}) fusion(bf16[768,2560]{1,0:T(8,128)(2,1)} %fusion.27, bf16[768,5120]{1,0:T(8,128)(2,1)} %all-gather.11.cloned.1.call-done.refs_1_, bf16[5120,2560]{1,0:T(8,128)(2,1)} %param.15), kind=kOutput, calls=%fused_computation.25 | convolution fusion | flops 20177879040 | bytes 45875200 | tf_op jit(solution)/shard_map/sh,hf->sf/dot_general | solution.py:17
  334.4 25.3 %convolution_convert_fusion.6 = bf16[768,5120]{1,0:T(8,128)(2,1)} fusion(bf16[768,2560]{1,0:T(8,128)(2,1)S(1)} %get-tuple-element.83.refs_3_, bf16[5120,2560]{1,0:T(8,128)(2,1)} %param.15), kind=kOutput, calls=%fused_computation.16 | convolution fusion | flops 20136591360 | bytes 38010880 | tf_op jit(solution)/shard_map/sf,hf->sh/dot_general | solution.py:17
  363.2 26.3 %convolution_convert_fusion.5 = bf16[768,5120]{1,0:T(8,128)(2,1)} fusion(bf16[768,2560]{1,0:T(8,128)(2,1)} %get-tuple-element.86.refs_0_, bf16[2560,5120]{1,0:T(8,128)(2,1)} %param.16), kind=kOutput, calls=%fused_computation.15 | convolution fusion | flops 20136591360 | bytes 38010880 | tf_op jit(solution)/shard_map/sf,fe->se/dot_general | solution.py:17
  389.6 26.3 %convolution_convert_fusion.4 = bf16[768,5120]{1,0:T(8,128)(2,1)} fusion(bf16[768,2560]{1,0:T(8,128)(2,1)} %get-tuple-element.85.refs_1_, bf16[2560,5120]{1,0:T(8,128)(2,1)} %param.16), kind=kOutput, calls=%fused_computation.14 | convolution fusion | flops 20136591360 | bytes 38010880 | tf_op jit(solution)/shard_map/sf,fe->se/dot_general | solution.py:17
  415.9 48.1 %d_down.1 = bf16[2560,5120]{1,0:T(8,128)(2,1)} custom-call(bf16[768,2560]{1,0:T(8,128)(2,1)} %get-tuple-element.86.refs_0_, bf16[768,2560]{1,0:T(8,128)(2,1)} %get-tuple-element.85.refs_1_, bf16[1536,5120]{1,0:T(8,128)(2,1)} %refs_3_.1, bf16[1536,5120]{1,0:T(8,128)(2,1)} %refs_3_.1), custom_call_target="tpu_custom_call" | custom-call | flops 40265318400 | bytes 49807360 | tf_op jit(solution)/shard_map/d_down/pallas_call | solution.py:205
  488.7 47.7 %d_up.1 = bf16[5120,2560]{1,0:T(8,128)(2,1)} custom-call(bf16[768,5120]{1,0:T(8,128)(2,1)} %all-gather.9.cloned.1.call-done.refs_0_, bf16[768,5120]{1,0:T(8,128)(2,1)} %all-gather.11.cloned.1.call-done.refs_1_, bf16[768,2560]{1,0:T(8,128)(2,1)} %copy-done.5, bf16[768,2560]{1,0:T(8,128)(2,1)} %copy-done.6), custom_call_target="tpu_custom_call" | custom-call | flops 40265318400 | bytes 49807360 | tf_op jit(solution)/shard_map/d_up/pallas_call | solution.py:205
  547.9 22.5 %attn_bwd_1.1 = (bf16[768,1920]{1,0:T(8,128)(2,1)}, f32[768,1280]{1,0:T(8,128)}) custom-call(s32[1536,256]{1,0:T(8,128)} %broadcast_in_dim.15.refs_0_, s32[1,1536]{1,0:T(1,128)} %broadcast_in_dim.16.refs_1_, bf16[768,1920]{1,0:T(8,128)(2,1)} %convolution_convert_fusion.9.refs_2_, bf16[768,1920]{1,0:T(8,128)(2,1)} %convolution_convert_fusion.8.refs_3_, ...), custom_call_target="tpu_custom_call" | custom-call | flops 11324620800 | bytes 5898240 | tf_op jit(solution)/shard_map/attn_bwd_1/pallas_call | solution.py:177
  570.4 23.2 %convolution_convert_fusion.3 = bf16[768,5120]{1,0:T(8,128)(2,1)} fusion(bf16[768,1920]{1,0:T(8,128)(2,1)} %get-tuple-element.96.refs_3_, bf16[5120,1920]{1,0:T(8,128)(2,1)} %param.13), kind=kOutput, calls=%fused_computation.13 | convolution fusion | flops 15103426560 | bytes 30474240 | tf_op jit(solution)/shard_map/sc,hc->sh/dot_general | solution.py:17
  617.2 23.2 %convolution_convert_fusion.2 = bf16[768,5120]{1,0:T(8,128)(2,1)} fusion(bf16[768,1920]{1,0:T(8,128)(2,1)} %attn_bwd_0.1.refs_2_, bf16[5120,1920]{1,0:T(8,128)(2,1)} %param.13), kind=kOutput, calls=%fused_computation.12 | convolution fusion | flops 15103426560 | bytes 30474240 | tf_op jit(solution)/shard_map/sc,hc->sh/dot_general | solution.py:17
  661.7 45.7 %reduce-scatter.19.cloned.1.call-done.d_ref = bf16[96,5120]{1,0:T(8,128)(2,1)} async-done(((bf16[768,5120]{1,0:T(8,128)(2,1)}), bf16[96,5120]{1,0:T(8,128)(2,1)}) %reduce-scatter.19.cloned.1.call-update) | async-done | bytes 983056 | tf_op jit(solution)/shard_map/reduce_scatter | solution.py:282
  712.3 58.7 %reduce-scatter.21.cloned.1.call-done.sum_ref = bf16[96,5120]{1,0:T(8,128)(2,1)} async-done(((bf16[768,5120]{1,0:T(8,128)(2,1)}), bf16[96,5120]{1,0:T(8,128)(2,1)}) %reduce-scatter.21.cloned.1.call-update) | async-done | bytes 983056 | tf_op jit(solution)/shard_map/reduce_scatter | solution.py:282
  773.7 39.3 %d_wqkv.1 = bf16[5120,1920]{1,0:T(8,128)(2,1)} custom-call(bf16[768,5120]{1,0:T(8,128)(2,1)} %ln1_0.1.refs_0_, bf16[768,5120]{1,0:T(8,128)(2,1)} %ln1_1.1.refs_1_, bf16[768,1920]{1,0:T(8,128)(2,1)} %attn_bwd_0.1.refs_2_, bf16[768,1920]{1,0:T(8,128)(2,1)} %get-tuple-element.96.refs_3_), custom_call_target="tpu_custom_call" | custom-call | flops 30198988800 | bytes 41287680 | tf_op jit(solution)/shard_map/d_wqkv/pallas_call | solution.py:205
  813.0 21.6 %reduce-scatter.23.cloned.1.call-done.d_ref = bf16[96,5120]{1,0:T(8,128)(2,1)} async-done(((bf16[768,5120]{1,0:T(8,128)(2,1)}), bf16[96,5120]{1,0:T(8,128)(2,1)}) %reduce-scatter.23.cloned.1.call-update) | async-done | bytes 983056 | tf_op jit(solution)/shard_map/reduce_scatter | solution.py:282
  842.2 22.9 %psum.7 = bf16[2,5120]{1,0:T(2,128)(2,1)S(1)} all-reduce(f32[2,5120]{1,0:T(2,128)S(1)} %pad_maximum_fusion.2), channel_id=1, replica_groups=mesh['data'=1,'model'=8] {'model'}, use_global_device_ids=true, to_apply=%region_8.0 | all-reduce | flops 10240 | bytes 61440 | tf_op jit(solution)/shard_map/psum | solution.py:360
  886.6 47.8 %all-gather.23.cloned.1.call-done = bf16[768,5120]{1,0:T(8,128)(2,1)} async-done(((bf16[96,5120]{1,0:T(8,128)(2,1)}), bf16[768,5120]{1,0:T(8,128)(2,1)}) %all-gather.23.cloned.1.call-update) | async-done | bytes 7864336 | tf_op jit(solution)/shard_map/all_gather | solution.py:285
  947.7 34.6 %all-gather.17.cloned.1.call-done = bf16[768,5120]{1,0:T(8,128)(2,1)} async-done(((bf16[96,5120]{1,0:T(8,128)(2,1)}), bf16[768,5120]{1,0:T(8,128)(2,1)}) %all-gather.17.cloned.1.call-update) | async-done | bytes 7864336 | tf_op jit(solution)/shard_map/all_gather | solution.py:285
  982.3 47.8 %all-gather.19.cloned.1.call-done = bf16[768,5120]{1,0:T(8,128)(2,1)} async-done(((bf16[96,5120]{1,0:T(8,128)(2,1)}), bf16[768,5120]{1,0:T(8,128)(2,1)}) %all-gather.19.cloned.1.call-update) | async-done | bytes 7864336 | tf_op jit(solution)/shard_map/all_gather | solution.py:285
  (85 shorter events, 240.6 us)
Async XLA Ops:
  7.2 146.7 %reduce-scatter.9.cloned.1.call-start = ((), (), s32[]{:S(2)}) async-start(), calls=%async_computation.8 | async-start | bytes 8847360 | tf_op jit(solution)/shard_map/reduce_scatter | solution.py:282
  20.5 22.6 %copy-start = (s32[1536]{0:T(1024)S(1)}, s32[1536]{0:T(1024)}, u32[]{:S(2)}) copy-start(s32[1536]{0:T(1024)} %param.10) | copy-start | bytes 18436
  64.5 127.6 %reduce-scatter.11.cloned.1.call-start = ((), (), s32[]{:S(2)}) async-start(), calls=%async_computation.9 | async-start | bytes 8847360 | tf_op jit(solution)/shard_map/reduce_scatter | solution.py:282
  122.9 117.7 %all-gather.9.cloned.1.call-start = ((), (), s32[]{:S(2)}) async-start(), calls=%async_computation.10 | async-start | bytes 8847360 | tf_op jit(solution)/shard_map/all_gather | solution.py:285
  123.3 29.9 %copy-start.4 = (bf16[5120]{0:T(1024)(128)(2,1)S(1)}, bf16[5120]{0:T(1024)(128)(2,1)}, u32[]{:S(2)}) copy-start(bf16[5120]{0:T(1024)(128)(2,1)} %param.12) | copy-start | bytes 30724
  157.5 142.7 %all-gather.11.cloned.1.call-start = ((), (), s32[]{:S(2)}) async-start(), calls=%async_computation.11 | async-start | bytes 8847360 | tf_op jit(solution)/shard_map/all_gather | solution.py:285
  195.7 268.3 %reduce-scatter.13.cloned.1.call-start = ((), (), s32[]{:S(2)}) async-start(), calls=%async_computation.12 | async-start | bytes 8847360 | tf_op jit(solution)/shard_map/reduce_scatter | solution.py:282
  273.0 1.9 copy-start.5
  332.4 2.0 copy-start.6
  359.7 124.0 %reduce-scatter.15.cloned.1.call-start = ((), (), s32[]{:S(2)}) async-start(), calls=%async_computation.13 | async-start | bytes 8847360 | tf_op jit(solution)/shard_map/reduce_scatter | solution.py:282
  360.2 176.2 %all-gather.15.cloned.1.call-start = ((), (), s32[]{:S(2)}) async-start(), calls=%async_computation.15 | async-start | bytes 8847360 | tf_op jit(solution)/shard_map/all_gather | solution.py:285
  469.0 124.8 %all-gather.13.cloned.1.call-start = ((), (), s32[]{:S(2)}) async-start(), calls=%async_computation.14 | async-start | bytes 8847360 | tf_op jit(solution)/shard_map/all_gather | solution.py:285
  488.7 155.2 %reduce-scatter.17.cloned.1.call-start = ((), (), s32[]{:S(2)}) async-start(), calls=%async_computation.16 | async-start | bytes 8847360 | tf_op jit(solution)/shard_map/reduce_scatter | solution.py:282
  547.8 159.6 %reduce-scatter.19.cloned.1.call-start = ((), (), s32[]{:S(2)}) async-start(), calls=%async_computation.17 | async-start | bytes 8847360 | tf_op jit(solution)/shard_map/reduce_scatter | solution.py:282
  593.7 177.4 %reduce-scatter.21.cloned.1.call-start = ((), (), s32[]{:S(2)}) async-start(), calls=%async_computation.18 | async-start | bytes 8847360 | tf_op jit(solution)/shard_map/reduce_scatter | solution.py:282
  605.1 229.5 %reduce-scatter.23.cloned.1.call-start = ((), (), s32[]{:S(2)}) async-start(), calls=%async_computation.21 | async-start | bytes 8847360 | tf_op jit(solution)/shard_map/reduce_scatter | solution.py:282
  640.4 246.2 %all-gather.21.cloned.1.call-start = ((), (), s32[]{:S(2)}) async-start(), calls=%async_computation.22 | async-start | bytes 8847360 | tf_op jit(solution)/shard_map/all_gather | solution.py:285
  773.7 67.6 %copy-start.1 = (f32[1,5120]{1,0:T(1,128)S(1)}, f32[1,5120]{1,0:T(1,128)}, u32[]{:S(2)}) copy-start(f32[1,5120]{1,0:T(1,128)} %get-tuple-element.115) | copy-start | bytes 61444
  773.7 67.6 %copy-start.2 = (f32[1,5120]{1,0:T(1,128)S(1)}, f32[1,5120]{1,0:T(1,128)}, u32[]{:S(2)}) copy-start(f32[1,5120]{1,0:T(1,128)} %get-tuple-element.114) | copy-start | bytes 61444
  773.7 67.6 %copy-start.3 = (f32[1,5120]{1,0:T(1,128)S(1)}, f32[1,5120]{1,0:T(1,128)}, u32[]{:S(2)}) copy-start(f32[1,5120]{1,0:T(1,128)} %get-tuple-element.113) | copy-start | bytes 61444
  839.6 94.9 %all-gather.23.cloned.1.call-start = ((), (), s32[]{:S(2)}) async-start(), calls=%async_computation.23 | async-start | bytes 8847360 | tf_op jit(solution)/shard_map/all_gather | solution.py:285
  840.2 142.2 %all-gather.17.cloned.1.call-start = ((), (), s32[]{:S(2)}) async-start(), calls=%async_computation.19 | async-start | bytes 8847360 | tf_op jit(solution)/shard_map/all_gather | solution.py:285
  840.7 189.4 %all-gather.19.cloned.1.call-start = ((), (), s32[]{:S(2)}) async-start(), calls=%async_computation.20 | async-start | bytes 8847360 | tf_op jit(solution)/shard_map/all_gather | solution.py:285
Sparse Core Ops, SparseCore 0:
  64.6 63.1 reduce-scatter.8
  131.7 60.2 reduce-scatter.10
  194.4 46.1 all-gather.8
  242.9 46.1 all-gather.10
  359.8 60.3 reduce-scatter.12
  423.4 60.2 reduce-scatter.14
  485.5 46.0 all-gather.14
  533.4 46.1 all-gather.12
  583.6 60.2 reduce-scatter.16
  647.1 60.2 reduce-scatter.18
  710.8 60.2 reduce-scatter.20
  774.3 60.2 reduce-scatter.22
  839.7 46.9 all-gather.20
  888.3 46.1 all-gather.22
  936.1 46.1 all-gather.16
  984.0 46.1 all-gather.18
